TPU v7x, 32 devices: a whole 2x2x4 slice. The times are simulated.
32 devices in a mesh: seq: 16 (over z, y, x), dp: 2 (over core).
Axes of the slice: x: 2, y: 2, z: 4, core: 2. Of those that a mesh axis runs over, the one named last changes fastest.
Arguments:
- queries: bfloat16 [2, 3072, 4096], P('dp', 'seq'), may hold values from -6 to 6
- key_vectors: bfloat16 [2, 3072, 4096], P('dp', 'seq'), may hold values from -0.52734375 to 0.52734375
- value_vectors: bfloat16 [2, 3072, 4096], P('dp', 'seq'), may hold values from -6 to 6
- out_grad: bfloat16 [2, 3072, 4096], P('dp', 'seq'), may hold values from -8 to 8
- log_decay: float32 [2, 32, 3072], P('dp', None, 'seq'), may hold values from -0.7729167 to 0, as said below
- norm_gain: float32 [4096], replicated, may hold values from 0.25 to 1.75
Outputs:
- output: bfloat16 [2, 3072, 4096], P('dp', 'seq')
- grad_queries: bfloat16 [2, 3072, 4096], P('dp', 'seq')
- grad_keys: bfloat16 [2, 3072, 4096], P('dp', 'seq')
- grad_values: bfloat16 [2, 3072, 4096], P('dp', 'seq')
- grad_gain: float32 [4096], P('seq')
Inputs may be any that keep to these rules, and one draw needn't show every extreme that they name: `log_decay`: every entry is negative.
All inputs are finite; a program needn't handle non-finite values.
Results may differ from a plain program's by a relative error of at most 0.006.
Values may be sent and summed in bfloat16 or wider, within the bound.
A program may use at most 128 MiB of HBM per device.

v0:
```python
import jax
import jax.numpy as jnp
from jax import lax
from jax.sharding import PartitionSpec as P

epsilon = 1e-06


def partner_2(value, axis, distance):
    mask = 2**distance
    pairs = [(source, source ^ mask) for source in range(lax.axis_size(axis))]
    return lax.ppermute(value, axis, pairs)


def combine(earlier, later):
    return (earlier[0] * later[0], later[0][..., None, None] * earlier[1] + later[1])


def pick(flag, first, second):
    return (jnp.where(flag, first[0], second[0]), jnp.where(flag, first[1], second[1]))


def forward_prefix(pair, identity):
    levels = lax.axis_size("seq").bit_length() - 1
    window = pair
    before = identity
    index = lax.axis_index("seq")
    for level in range(levels):
        partner = partner_2((window[0], window[1]), "seq", level)
        lower = index >> level & 1 == 1
        before = pick(lower, combine(partner, before), before)
        window = pick(lower, combine(partner, window), combine(window, partner))
    return before[1]


def backward_prefix(pair, identity):
    levels = lax.axis_size("seq").bit_length() - 1
    window = pair
    before = identity
    index = lax.axis_index("seq")
    for level in range(levels):
        partner = partner_2((window[0], window[1]), "seq", level)
        higher = index >> level & 1 == 0
        before = pick(higher, combine(partner, before), before)
        window = pick(higher, combine(partner, window), combine(window, partner))
    return before[1]


def body(queries, key_vectors, value_vectors, out_grad, log_decay, norm_gain):
    local_seqs, tokens, feature_count = queries.shape
    head_count = log_decay.shape[1]
    head_size = feature_count // head_count
    sequence_partition = (local_seqs, tokens, head_count, head_size)
    query_heads = queries.reshape(sequence_partition)
    key_heads = key_vectors.reshape(sequence_partition)
    value_heads = value_vectors.reshape(sequence_partition)
    cumulative = jnp.cumsum(log_decay, axis=2)
    block_total = cumulative[:, :, -1]
    positions = jnp.arange(tokens)
    causal = positions[:, None] >= positions[None, :]
    log_gap = cumulative[:, :, :, None] - cumulative[:, :, None, :]
    weight = jnp.where(causal, jnp.exp(jnp.where(causal, log_gap, 0.0)), 0.0)
    start_scale = jnp.exp(cumulative).transpose(0, 2, 1)[..., None]
    end_scale = jnp.exp(block_total[:, :, None] - cumulative).transpose(0, 2, 1)[..., None]
    decay_total = jnp.exp(block_total)
    key_decayed = (key_heads * end_scale).astype(jnp.bfloat16)
    local_state = jnp.einsum(
        "sjhd,sjhe->shde", key_decayed, value_heads, preferred_element_type=jnp.float32
    )
    identity = (jnp.ones_like(decay_total), jnp.zeros_like(local_state))
    prior_state = forward_prefix((decay_total, local_state), identity).astype(jnp.bfloat16)
    scores = jnp.einsum(
        "sihe,sjhe->shij", query_heads, key_heads, preferred_element_type=jnp.float32
    )
    weighted = (scores * weight).astype(jnp.bfloat16)
    inside = jnp.einsum(
        "shij,sjhe->sihe", weighted, value_heads, preferred_element_type=jnp.float32
    )
    carried = (
        jnp.einsum("sihd,shde->sihe", query_heads, prior_state, preferred_element_type=jnp.float32)
        * start_scale
    )
    attended = inside + carried
    inv_rms = lax.rsqrt(jnp.mean(attended * attended, axis=-1, keepdims=True) + epsilon)
    normed = attended * inv_rms
    gain_heads = norm_gain.reshape(head_count, head_size)
    output = (normed * gain_heads).astype(jnp.bfloat16).reshape(queries.shape)
    grad_out = out_grad.reshape(sequence_partition).astype(jnp.float32)
    scaled = grad_out * gain_heads
    grad_attended = (
        inv_rms * (scaled - normed * jnp.mean(scaled * normed, axis=-1, keepdims=True))
    ).astype(jnp.bfloat16)
    gain_term = jnp.sum(grad_out * normed, axis=(0, 1)).reshape(feature_count)
    query_decayed = (query_heads * start_scale).astype(jnp.bfloat16)
    later_local = jnp.einsum(
        "sihd,sihe->shde", query_decayed, grad_attended, preferred_element_type=jnp.float32
    )
    later_state = backward_prefix((decay_total, later_local), identity).astype(jnp.bfloat16)
    grad_scores = jnp.einsum(
        "sihe,sjhe->shij", grad_attended, value_heads, preferred_element_type=jnp.float32
    )
    grad_weighted = (grad_scores * weight).astype(jnp.bfloat16)
    grad_query = jnp.einsum(
        "shij,sjhd->sihd", grad_weighted, key_heads, preferred_element_type=jnp.float32
    )
    grad_query = grad_query + start_scale * jnp.einsum(
        "sihe,shde->sihd", grad_attended, prior_state, preferred_element_type=jnp.float32
    )
    grad_key = jnp.einsum(
        "shij,sihd->sjhd", grad_weighted, query_heads, preferred_element_type=jnp.float32
    )
    grad_key = grad_key + end_scale * jnp.einsum(
        "sjhe,shde->sjhd", value_heads, later_state, preferred_element_type=jnp.float32
    )
    grad_value = jnp.einsum(
        "shij,sihe->sjhe", weighted, grad_attended, preferred_element_type=jnp.float32
    )
    grad_value = grad_value + end_scale * jnp.einsum(
        "sjhd,shde->sjhe", key_heads, later_state, preferred_element_type=jnp.float32
    )
    summed = lax.psum(gain_term, "dp")
    grad_gain = lax.psum_scatter(summed, "seq", scatter_dimension=0, tiled=True)
    return (
        output,
        grad_query.astype(jnp.bfloat16).reshape(queries.shape),
        grad_key.astype(jnp.bfloat16).reshape(queries.shape),
        grad_value.astype(jnp.bfloat16).reshape(queries.shape),
        grad_gain,
    )


def solution(mesh):
    in_specs = (
        P("dp", "seq", None),
        P("dp", "seq", None),
        P("dp", "seq", None),
        P("dp", "seq", None),
        P("dp", None, "seq"),
        P(),
    )
    out_specs = (
        P("dp", "seq", None),
        P("dp", "seq", None),
        P("dp", "seq", None),
        P("dp", "seq", None),
        P("seq"),
    )
    return jax.shard_map(body, mesh=mesh, in_specs=in_specs, out_specs=out_specs, check_vma=False)
```

profile of v0, /device:TPU:0, one launch (start us, length us, event | category | flops | bytes accessed | tf_op | source)
XLA Modules:
  0.0 598.5 jit_solution(130886182880386030)
XLA Ops:
  3.1 1.7 copy.112
  5.2 5.7 fusion.11
  10.9 3.0 collective-permute-start.3
  13.9 45.9 %collective-permute-done = f32[1,32]{1,0:T(1,128)S(1)} collective-permute-done((f32[1,32]{1,0:T(1,128)S(1)}, f32[1,32]{1,0:T(1,128)S(1)}, u32[]{:S(2)}, u32[]{:S(2)}) %collective-permute-start) | collective-permute-done | bytes 160 | tf_op jit(solution)/shard_map/ppermute | solution.py:12
  59.9 4.1 fusion.10
  63.9 1.8 collective-permute-start.4
  66.0 45.1 %collective-permute-done.1 = f32[1,32]{1,0:T(1,128)S(1)} collective-permute-done((f32[1,32]{1,0:T(1,128)S(1)}, f32[1,32]{1,0:T(1,128)S(1)}, u32[]{:S(2)}, u32[]{:S(2)}) %collective-permute-start.1) | collective-permute-done | bytes 160 | tf_op jit(solution)/shard_map/ppermute | solution.py:12
  111.1 4.1 add_select_fusion.9
  117.2 44.2 %collective-permute-done.2 = f32[1,32]{1,0:T(1,128)S(1)} collective-permute-done((f32[1,32]{1,0:T(1,128)S(1)}, f32[1,32]{1,0:T(1,128)S(1)}, u32[]{:S(2)}, u32[]{:S(2)}) %collective-permute-start.2) | collective-permute-done | bytes 160 | tf_op jit(solution)/shard_map/ppermute | solution.py:12
  161.4 4.1 add_select_fusion.8
  165.5 2.3 collective-permute-start.6
  167.8 1.9 copy.111
  170.6 4.5 multiply_convert_fusion.1
  176.8 79.9 %collective-permute-done.6 = f32[1,32,128,128]{3,2,1,0:T(8,128)} collective-permute-done((f32[1,32,128,128]{3,2,1,0:T(8,128)}, f32[1,32,128,128]{3,2,1,0:T(8,128)}, u32[]{:S(2)}, u32[]{:S(2)}) %collective-permute-start.6) | collective-permute-done | bytes 2097184 | tf_op jit(solution)/shard_map/ppermute | solution.py:12
  256.8 4.7 fusion.7
  261.5 3.7 multiply_reduce_fusion.2
  265.2 5.0 multiply_reduce_fusion
  270.3 4.5 fusion.13
  274.8 3.2 fusion.14
  279.6 45.6 %collective-permute-done.7 = f32[1,32,128,128]{3,2,1,0:T(8,128)S(1)} collective-permute-done((f32[1,32,128,128]{3,2,1,0:T(8,128)S(1)}, f32[1,32,128,128]{3,2,1,0:T(8,128)S(1)}, u32[]{:S(2)}, u32[]{:S(2)}) %collective-permute-start.7) | collective-permute-done | bytes 2097184 | tf_op jit(solution)/shard_map/ppermute | solution.py:12
  327.2 45.6 %collective-permute-done.8 = f32[1,32,128,128]{3,2,1,0:T(8,128)S(1)} collective-permute-done((f32[1,32,128,128]{3,2,1,0:T(8,128)S(1)}, f32[1,32,128,128]{3,2,1,0:T(8,128)S(1)}, u32[]{:S(2)}, u32[]{:S(2)}) %collective-permute-start.8) | collective-permute-done | bytes 2097184 | tf_op jit(solution)/shard_map/ppermute | solution.py:12
  372.8 2.0 add_select_fusion.7
  377.6 112.0 %all-reduce.1 = f32[4096]{0:T(1024)S(1)} all-reduce(f32[4096]{0:T(1024)S(1)} %bitcast.200), channel_id=2, replica_groups=mesh['seq'=16,'dp'=2] {'seq'}, use_global_device_ids=true, to_apply=%region_6.7.clone | all-reduce | flops 4096 | bytes 32768
  489.7 3.0 psum.8
  492.7 3.4 multiply_convert_fusion
  497.2 2.7 add_select_fusion.6
  504.9 2.1 copy_bitcast_fusion.2
  507.0 81.2 %collective-permute-done.10 = f32[1,32,128,128]{3,2,1,0:T(8,128)S(1)} collective-permute-done((f32[1,32,128,128]{3,2,1,0:T(8,128)S(1)}, f32[1,32,128,128]{3,2,1,0:T(8,128)S(1)}, u32[]{:S(2)}, u32[]{:S(2)}) %collective-permute-start.10) | collective-permute-done | bytes 2097184 | tf_op jit(solution)/shard_map/ppermute | solution.py:12
  588.2 3.5 fusion.8
  591.7 2.3 fusion.19
  594.0 2.3 fusion.18
  596.3 2.1 copy_bitcast_fusion
  (78 shorter events, 19.4 us)
Async XLA Ops:
  2.3 2.6 copy-start.13
  4.9 165.8 %copy-start = (bf16[24,8,32,128]{3,2,1,0:T(8,128)(2,1)}, bf16[24,8,32,128]{3,2,1,0:T(8,128)(2,1)S(1)}, u32[]{:S(2)}) copy-start(bf16[24,8,32,128]{3,2,1,0:T(8,128)(2,1)S(1)} %copy.112) | copy-start | bytes 4718596
  10.9 48.9 %collective-permute-start.3 = (f32[1,32,128,128]{3,2,1,0:T(8,128)}, f32[1,32,128,128]{3,2,1,0:T(8,128)}, u32[]{:S(2)}, u32[]{:S(2)}) collective-permute-start(f32[1,32,128,128]{3,2,1,0:T(8,128)} %bitcast.10), channel_id=1, source_target_pairs={{0,2},{2,0},{4,6},{6,4},{8,10},{10,8},{12,14},{14,12},{16,18},{18,... | collective-permute-start | bytes 6291464 | tf_op jit(solution)/shard_map/ppermute | solution.py:12
  13.9 45.9 %collective-permute-start = (f32[1,32]{1,0:T(1,128)S(1)}, f32[1,32]{1,0:T(1,128)S(1)}, u32[]{:S(2)}, u32[]{:S(2)}) collective-permute-start(f32[1,32]{1,0:T(1,128)S(1)} %bitcast.216), channel_id=1, source_target_pairs={{0,2},{2,0},{4,6},{6,4},{8,10},{10,8},{12,14},{14,12},{16,18},{18,... | collective-permute-start | bytes 392 | tf_op jit(solution)/shard_map/ppermute | solution.py:12
  63.9 47.1 %collective-permute-start.4 = (f32[1,32,128,128]{3,2,1,0:T(8,128)}, f32[1,32,128,128]{3,2,1,0:T(8,128)}, u32[]{:S(2)}, u32[]{:S(2)}) collective-permute-start(f32[1,32,128,128]{3,2,1,0:T(8,128)} %fusion.10), channel_id=1, source_target_pairs={{0,4},{2,6},{4,0},{6,2},{8,12},{10,14},{12,8},{14,10},{16,20},{18,... | collective-permute-start | bytes 6291464 | tf_op jit(solution)/shard_map/ppermute | solution.py:12
  65.7 45.3 %collective-permute-start.1 = (f32[1,32]{1,0:T(1,128)S(1)}, f32[1,32]{1,0:T(1,128)S(1)}, u32[]{:S(2)}, u32[]{:S(2)}) collective-permute-start(f32[1,32]{1,0:T(1,128)S(1)} %bitcast_multiply_fusion.4), channel_id=1, source_target_pairs={{0,4},{2,6},{4,0},{6,2},{8,12},{10,14},{12,8},{14,10},{16,20},{18,... | collective-permute-start | bytes 392 | tf_op jit(solution)/shard_map/ppermute | solution.py:12
  115.1 46.3 %collective-permute-start.5 = (f32[1,32,128,128]{3,2,1,0:T(8,128)}, f32[1,32,128,128]{3,2,1,0:T(8,128)}, u32[]{:S(2)}, u32[]{:S(2)}) collective-permute-start(f32[1,32,128,128]{3,2,1,0:T(8,128)} %add_select_fusion.9), channel_id=1, source_target_pairs={{0,8},{2,10},{4,12},{6,14},{8,0},{10,2},{12,4},{14,6},{16,24},{18,... | collective-permute-start | bytes 6291464 | tf_op jit(solution)/shard_map/ppermute | solution.py:12
  116.7 44.7 %collective-permute-start.2 = (f32[1,32]{1,0:T(1,128)S(1)}, f32[1,32]{1,0:T(1,128)S(1)}, u32[]{:S(2)}, u32[]{:S(2)}) collective-permute-start(f32[1,32]{1,0:T(1,128)S(1)} %mul.303), channel_id=1, source_target_pairs={{0,8},{2,10},{4,12},{6,14},{8,0},{10,2},{12,4},{14,6},{16,24},{18,... | collective-permute-start | bytes 392 | tf_op jit(solution)/shard_map/ppermute | solution.py:12
  165.5 91.3 %collective-permute-start.6 = (f32[1,32,128,128]{3,2,1,0:T(8,128)}, f32[1,32,128,128]{3,2,1,0:T(8,128)}, u32[]{:S(2)}, u32[]{:S(2)}) collective-permute-start(f32[1,32,128,128]{3,2,1,0:T(8,128)} %add_select_fusion.8), channel_id=1, source_target_pairs={{0,16},{2,18},{4,20},{6,22},{8,24},{10,26},{12,28},{14,30},{16,0},... | collective-permute-start | bytes 6291464 | tf_op jit(solution)/shard_map/ppermute | solution.py:12
  167.8 1.9 copy-start.14
  169.7 105.1 %copy-start.2 = (bf16[24,8,32,128]{3,2,1,0:T(8,128)(2,1)}, bf16[24,8,32,128]{3,2,1,0:T(8,128)(2,1)S(1)}, u32[]{:S(2)}) copy-start(bf16[24,8,32,128]{3,2,1,0:T(8,128)(2,1)S(1)} %copy.111) | copy-start | bytes 4718596
  175.2 1.7 copy-start.4
  261.5 3.7 copy-start.6
  261.5 3.7 copy-start.15
  278.0 47.2 %collective-permute-start.7 = (f32[1,32,128,128]{3,2,1,0:T(8,128)S(1)}, f32[1,32,128,128]{3,2,1,0:T(8,128)S(1)}, u32[]{:S(2)}, u32[]{:S(2)}) collective-permute-start(f32[1,32,128,128]{3,2,1,0:T(8,128)S(1)} %bitcast.186), channel_id=1, source_target_pairs={{0,2},{2,0},{4,6},{6,4},{8,10},{10,8},{12,14},{14,12},{16,18},{18,... | collective-permute-start | bytes 6291464 | tf_op jit(solution)/shard_map/ppermute | solution.py:12
  325.2 1.3 copy-start.8
  326.5 49.9 %copy-start.16 = (u32[32]{0:T(128)S(1)}, u32[32]{0:T(128)}, u32[]{:S(2)}) copy-start(u32[32]{0:T(128)} %constant.37) | copy-start | bytes 388
  326.5 46.3 %collective-permute-start.8 = (f32[1,32,128,128]{3,2,1,0:T(8,128)S(1)}, f32[1,32,128,128]{3,2,1,0:T(8,128)S(1)}, u32[]{:S(2)}, u32[]{:S(2)}) collective-permute-start(f32[1,32,128,128]{3,2,1,0:T(8,128)S(1)} %fusion.9), channel_id=1, source_target_pairs={{0,4},{2,6},{4,0},{6,2},{8,12},{10,14},{12,8},{14,10},{16,20},{18,... | collective-permute-start | bytes 6291464 | tf_op jit(solution)/shard_map/ppermute | solution.py:12
  372.8 2.0 copy-start.10
  374.9 122.3 %collective-permute-start.9 = (f32[1,32,128,128]{3,2,1,0:T(8,128)}, f32[1,32,128,128]{3,2,1,0:T(8,128)}, u32[]{:S(2)}, u32[]{:S(2)}) collective-permute-start(f32[1,32,128,128]{3,2,1,0:T(8,128)} %add_select_fusion.7), channel_id=1, source_target_pairs={{0,8},{2,10},{4,12},{6,14},{8,0},{10,2},{12,4},{14,6},{16,24},{18,... | collective-permute-start | bytes 6291464 | tf_op jit(solution)/shard_map/ppermute | solution.py:12
  492.7 3.4 copy-start.1
  497.2 2.9 copy-start.7
  500.0 1.9 copy-start.5
  500.0 88.2 %collective-permute-start.10 = (f32[1,32,128,128]{3,2,1,0:T(8,128)S(1)}, f32[1,32,128,128]{3,2,1,0:T(8,128)S(1)}, u32[]{:S(2)}, u32[]{:S(2)}) collective-permute-start(f32[1,32,128,128]{3,2,1,0:T(8,128)S(1)} %add_select_fusion.6), channel_id=1, source_target_pairs={{0,16},{2,18},{4,20},{6,22},{8,24},{10,26},{12,28},{14,30},{16,0},... | collective-permute-start | bytes 6291464 | tf_op jit(solution)/shard_map/ppermute | solution.py:12
  501.9 1.4 copy-start.3
  503.3 1.6 copy-start.12
  504.9 83.3 %copy-start.9 = (f32[1,32,128,128]{3,2,1,0:T(8,128)S(1)}, f32[1,32,128,128]{3,2,1,0:T(8,128)}, u32[]{:S(2)}) copy-start(f32[1,32,128,128]{3,2,1,0:T(8,128)} %copy-done.8) | copy-start | bytes 6291460
  504.9 83.3 %copy-start.11 = (f32[1,32,128,128]{3,2,1,0:T(8,128)S(1)}, f32[1,32,128,128]{3,2,1,0:T(8,128)}, u32[]{:S(2)}) copy-start(f32[1,32,128,128]{3,2,1,0:T(8,128)} %copy-done.10) | copy-start | bytes 6291460
where the time goes:
time: 599 us; the launch traced here: 598 us
  waiting for transfers between devices  388 us (65%)
  blocking collectives  115 us (19%)
  other arithmetic  36.4 us (6%)
  matrix products  31.2 us (5%)
  local copies, waits for them, and re-layouts  13.4 us (2%)
  starting transfers between devices  13.2 us (2%)
    ppermute x11, waiting for transfers between devices, partner_2(): return lax.ppermute(value, axis, pairs)  388 us
    unnamed x1, blocking collectives  112 us
    select_n x6, other arithmetic, pick(): jnp.where(flag, first[1], second[1])  17.5 us
    ppermute x11, starting transfers between devices, partner_2(): return lax.ppermute(value, axis, pairs)  13.2 us
  transfers between devices with their start and end apart: 11, of which 7 were waited for; matrix products, arithmetic and copies ran while one was open for 3% of the time, Pallas kernels for 0%

commit v1 on v0

v1 whole, which is shorter than its diff:
```python
import functools

import jax
import jax.numpy as jnp
from jax import lax
from jax.experimental import pallas as pl
from jax.experimental.pallas import tpu as pltpu
from jax.sharding import PartitionSpec as P

epsilon = 1e-06
F32 = jnp.float32
BF16 = jnp.bfloat16
MESH = pl.DeviceIdType.MESH
NEG = -1e30


def dot_nn(a, b):
    return lax.dot_general(a, b, (((1,), (0,)), ((), ())), preferred_element_type=F32)


def dot_nt(a, b):
    return lax.dot_general(a, b, (((1,), (1,)), ((), ())), preferred_element_type=F32)


def dot_tn(a, b):
    return lax.dot_general(a, b, (((0,), (0,)), ((), ())), preferred_element_type=F32)


def cumulative(ld):
    tokens = ld.shape[1]
    i = lax.broadcasted_iota(jnp.int32, (tokens, tokens), 0)
    j = lax.broadcasted_iota(jnp.int32, (tokens, tokens), 1)
    lower = (i >= j).astype(F32)
    exact = lax.Precision.HIGHEST
    rows = lax.dot_general(
        ld, lower, (((1,), (1,)), ((), ())), precision=exact, preferred_element_type=F32
    )
    columns = lax.dot_general(
        lower, ld, (((1,), (1,)), ((), ())), precision=exact, preferred_element_type=F32
    )
    return rows, columns, i >= j


def local_kernel(heads, size, k_ref, v_ref, ld_ref, l_ref, a_ref):
    ld = ld_ref[0]
    rows, columns, _ = cumulative(ld)
    tokens = ld.shape[1]
    last = columns[tokens - 1 :, :]
    end = jnp.exp(last - columns)
    for h in range(heads):
        cols = slice(h * size, (h + 1) * size)
        kd = (k_ref[:, cols].astype(F32) * end[:, h : h + 1]).astype(BF16)
        l_ref[h] = dot_tn(kd, v_ref[:, cols]).astype(BF16)
        a_ref[0, h : h + 1, :] = jnp.broadcast_to(jnp.exp(last[:, h : h + 1]), (1, size))


def forward_kernel(
    heads, size, q_ref, k_ref, v_ref, g_ref, ld_ref, gain_ref, p_ref,
    out_ref, ga_ref, l_ref, term_ref,
):
    ld = ld_ref[0]
    rows, columns, causal = cumulative(ld)
    start = jnp.exp(columns)
    for h in range(heads):
        cols = slice(h * size, (h + 1) * size)
        q, k, v = q_ref[:, cols], k_ref[:, cols], v_ref[:, cols]
        weight = jnp.exp(jnp.where(causal, columns[:, h : h + 1] - rows[h : h + 1, :], NEG))
        weighted = (dot_nt(q, k) * weight).astype(BF16)
        begin = start[:, h : h + 1]
        attended = dot_nn(weighted, v) + dot_nn(q, p_ref[h]) * begin
        inv = lax.rsqrt(jnp.mean(attended * attended, axis=1, keepdims=True) + epsilon)
        normed = attended * inv
        gain = gain_ref[:, cols]
        out_ref[:, cols] = (normed * gain).astype(BF16)
        g = g_ref[:, cols].astype(F32)
        term_ref[0, h : h + 1, :] = jnp.sum(g * normed, axis=0, keepdims=True)
        scaled = g * gain
        ga = (inv * (scaled - normed * jnp.mean(scaled * normed, axis=1, keepdims=True))).astype(BF16)
        ga_ref[:, cols] = ga
        qd = (q.astype(F32) * begin).astype(BF16)
        l_ref[h] = dot_tn(qd, ga).astype(BF16)


def backward_kernel(
    heads, size, q_ref, k_ref, v_ref, ga_ref, ld_ref, p_ref, s_ref,
    gq_ref, gk_ref, gv_ref,
):
    ld = ld_ref[0]
    rows, columns, causal = cumulative(ld)
    tokens = ld.shape[1]
    start = jnp.exp(columns)
    end = jnp.exp(columns[tokens - 1 :, :] - columns)
    for h in range(heads):
        cols = slice(h * size, (h + 1) * size)
        q, k, v, ga = q_ref[:, cols], k_ref[:, cols], v_ref[:, cols], ga_ref[:, cols]
        weight = jnp.exp(jnp.where(causal, columns[:, h : h + 1] - rows[h : h + 1, :], NEG))
        weighted = (dot_nt(q, k) * weight).astype(BF16)
        gw = (dot_nt(ga, v) * weight).astype(BF16)
        begin, finish = start[:, h : h + 1], end[:, h : h + 1]
        gq_ref[:, cols] = (dot_nn(gw, k) + begin * dot_nt(ga, p_ref[h])).astype(BF16)
        gk_ref[:, cols] = (dot_tn(gw, q) + finish * dot_nt(v, s_ref[h])).astype(BF16)
        gv_ref[:, cols] = (dot_tn(weighted, ga) + finish * dot_nn(k, s_ref[h])).astype(BF16)


def scan_kernel(count, group, chunks, reverse, with_gain, *refs):
    if with_gain:
        (l_ref, a_ref, t_ref, p_ref, sum_ref, got, given, decay, carry_in, carry_out,
         got_send, got_recv, dec_send, dec_recv, car_send, car_recv, ret_send, ret_recv,
         gain_got, gain_send, gain_recv) = refs
    else:
        (l_ref, a_ref, p_ref, got, given, decay, carry_in, carry_out,
         got_send, got_recv, dec_send, dec_recv, car_send, car_recv, ret_send, ret_recv) = refs
    me = lax.axis_index("seq")
    dp = lax.axis_index("dp")
    planes = count // group
    mine = lax.rem(me, group)
    plane = me // group
    owned = l_ref.shape[0] // group
    piece = owned // chunks

    def owned_rows(peer, chunk):
        return pl.ds(peer * owned + chunk * piece, piece)

    def give_local(offset, chunk):
        peer = lax.rem(mine + offset, group)
        return pltpu.make_async_remote_copy(
            src_ref=l_ref.at[owned_rows(peer, chunk)],
            dst_ref=got.at[mine, pl.ds(chunk * piece, piece)],
            send_sem=got_send.at[offset, chunk],
            recv_sem=got_recv.at[offset, chunk],
            device_id=(plane * group + peer, dp),
            device_id_type=MESH,
        )

    def take_local(offset, chunk):
        peer = lax.rem(mine + group - offset, group)
        return pltpu.make_async_remote_copy(
            src_ref=l_ref.at[owned_rows(mine, chunk)],
            dst_ref=got.at[peer, pl.ds(chunk * piece, piece)],
            send_sem=got_send.at[offset, chunk],
            recv_sem=got_recv.at[offset, chunk],
            device_id=(plane * group + peer, dp),
            device_id_type=MESH,
        )

    def give_decay(offset):
        peer = lax.rem(mine + offset, group)
        return pltpu.make_async_remote_copy(
            src_ref=a_ref.at[pl.ds(peer * owned, owned)],
            dst_ref=decay.at[mine],
            send_sem=dec_send.at[offset],
            recv_sem=dec_recv.at[offset],
            device_id=(plane * group + peer, dp),
            device_id_type=MESH,
        )

    def take_decay(offset):
        peer = lax.rem(mine + group - offset, group)
        return pltpu.make_async_remote_copy(
            src_ref=a_ref.at[pl.ds(mine * owned, owned)],
            dst_ref=decay.at[peer],
            send_sem=dec_send.at[offset],
            recv_sem=dec_recv.at[offset],
            device_id=(plane * group + peer, dp),
            device_id_type=MESH,
        )

    def give_back(offset, chunk):
        peer = lax.rem(mine + offset, group)
        return pltpu.make_async_remote_copy(
            src_ref=given.at[peer, pl.ds(chunk * piece, piece)],
            dst_ref=p_ref.at[owned_rows(mine, chunk)],
            send_sem=ret_send.at[offset, chunk],
            recv_sem=ret_recv.at[offset, chunk],
            device_id=(plane * group + peer, dp),
            device_id_type=MESH,
        )

    def take_back(offset, chunk):
        peer = lax.rem(mine + group - offset, group)
        return pltpu.make_async_remote_copy(
            src_ref=given.at[mine, pl.ds(chunk * piece, piece)],
            dst_ref=p_ref.at[owned_rows(peer, chunk)],
            send_sem=ret_send.at[offset, chunk],
            recv_sem=ret_recv.at[offset, chunk],
            device_id=(plane * group + peer, dp),
            device_id_type=MESH,
        )

    step = planes - 1 if reverse else 1

    def carry(chunk):
        target = lax.rem(plane + step, planes) * group + mine
        return pltpu.make_async_remote_copy(
            src_ref=carry_out.at[pl.ds(chunk * piece, piece)],
            dst_ref=carry_in.at[pl.ds(chunk * piece, piece)],
            send_sem=car_send.at[chunk],
            recv_sem=car_recv.at[chunk],
            device_id=(target, dp),
            device_id_type=MESH,
        )

    first = plane == (planes - 1 if reverse else 0)
    final = plane == (0 if reverse else planes - 1)
    order = list(range(group))[::-1] if reverse else list(range(group))

    for offset in range(1, group):
        give_decay(offset).start()
    for chunk in range(chunks):
        for offset in range(1, group):
            give_local(offset, chunk).start()
    if with_gain:
        rows = gain_got.shape[1]
        total = 2 * count
        flat = me * 2 + dp

        def send_gain(offset, unused):
            there = lax.rem(flat + offset, total)
            pltpu.make_async_remote_copy(
                src_ref=t_ref.at[pl.ds((there // 2) * l_ref.shape[0] // count, rows)],
                dst_ref=gain_got.at[offset - 1],
                send_sem=gain_send,
                recv_sem=gain_recv,
                device_id=(there // 2, lax.rem(there, 2)),
                device_id_type=MESH,
            ).start()
            return unused

        lax.fori_loop(1, total, send_gain, 0)
    got[mine] = l_ref[pl.ds(mine * owned, owned)]
    decay[mine] = a_ref[pl.ds(mine * owned, owned)]

    @pl.when(first)
    def _():
        carry_in[...] = jnp.zeros_like(carry_in)

    for offset in range(1, group):
        take_decay(offset).wait_recv()
    for chunk in range(chunks):
        for offset in range(1, group):
            take_local(offset, chunk).wait_recv()

        @pl.when(jnp.logical_not(first))
        def _():
            carry(chunk).wait_recv()

        def combine(h, unused):
            value = carry_in[h].astype(F32)
            for g in order:
                given[g, h] = value.astype(BF16)
                value = decay[g, pl.ds(h, 1)] * value + got[g, h].astype(F32)
            carry_out[h] = value.astype(BF16)
            return unused

        lax.fori_loop(chunk * piece, (chunk + 1) * piece, combine, 0)

        @pl.when(jnp.logical_not(final))
        def _():
            carry(chunk).start()

        for offset in range(1, group):
            give_back(offset, chunk).start()
        p_ref[owned_rows(mine, chunk)] = given[mine, pl.ds(chunk * piece, piece)]

    if with_gain:
        everything = pltpu.make_async_copy(gain_got, gain_got, gain_recv)
        everything.wait()
        pltpu.make_async_copy(gain_got, gain_got, gain_send).wait()
        sum_ref[...] = jnp.sum(gain_got[...], axis=0) + t_ref[pl.ds(me * l_ref.shape[0] // count, rows)]

    for chunk in range(chunks):
        for offset in range(1, group):
            take_back(offset, chunk).wait_recv()
    for offset in range(1, group):
        give_decay(offset).wait_send()
        for chunk in range(chunks):
            give_local(offset, chunk).wait_send()
            give_back(offset, chunk).wait_send()

    @pl.when(jnp.logical_not(final))
    def _():
        for chunk in range(chunks):
            carry(chunk).wait_send()


def scan_call(count, states, decays, reverse, terms=None):
    heads, size, _ = states.shape
    group = 1 << ((count.bit_length()) // 2)
    owned = heads // group
    chunks = min(owned, 4)
    vmem = pl.BlockSpec(memory_space=pltpu.VMEM)
    dma = pltpu.SemaphoreType.DMA
    out_shape = [jax.ShapeDtypeStruct(states.shape, BF16)]
    args = [states, decays]
    scratch = [
        pltpu.VMEM((group, owned, size, size), BF16),
        pltpu.VMEM((group, owned, size, size), BF16),
        pltpu.VMEM((group, owned, size), F32),
        pltpu.VMEM((owned, size, size), BF16),
        pltpu.VMEM((owned, size, size), BF16),
        dma((group, chunks)),
        dma((group, chunks)),
        dma((group,)),
        dma((group,)),
        dma((chunks,)),
        dma((chunks,)),
        dma((group, chunks)),
        dma((group, chunks)),
    ]
    if terms is not None:
        rows = max(1, heads // count)
        args.append(terms)
        out_shape.append(jax.ShapeDtypeStruct((rows, size), F32))
        scratch += [pltpu.VMEM((2 * count - 1, rows, size), F32), dma, dma]
    return pl.pallas_call(
        functools.partial(scan_kernel, count, group, chunks, reverse, terms is not None),
        out_shape=out_shape,
        in_specs=[vmem] * len(args),
        out_specs=[vmem] * len(out_shape),
        scratch_shapes=scratch,
        compiler_params=pltpu.CompilerParams(
            has_side_effects=True, vmem_limit_bytes=48 * 1024 * 1024
        ),
        name="suffix_scan" if reverse else "prefix_scan",
    )(*args)


def body(count, queries, key_vectors, value_vectors, out_grad, log_decay, norm_gain):
    _, tokens, features = queries.shape
    heads = log_decay.shape[1]
    size = features // heads
    q, k, v, g = (x.reshape(tokens, features) for x in (queries, key_vectors, value_vectors, out_grad))
    per = 4
    steps = heads // per
    ld = log_decay.reshape(steps, per, tokens)
    gain = norm_gain.reshape(1, features)
    wide = pl.BlockSpec((tokens, per * size), lambda i: (0, i))
    decay_spec = pl.BlockSpec((1, per, tokens), lambda i: (i, 0, 0))
    state_spec = pl.BlockSpec((per, size, size), lambda i: (i, 0, 0))
    row_spec = pl.BlockSpec((1, per, size), lambda i: (i, 0, 0))
    gain_spec = pl.BlockSpec((1, per * size), lambda i: (0, i))
    wide_shape = jax.ShapeDtypeStruct((tokens, features), BF16)
    state_shape = jax.ShapeDtypeStruct((heads, size, size), BF16)
    row_shape = jax.ShapeDtypeStruct((steps, per, size), F32)
    params = pltpu.CompilerParams(vmem_limit_bytes=48 * 1024 * 1024)

    local_state, decays = pl.pallas_call(
        functools.partial(local_kernel, per, size),
        grid=(steps,),
        in_specs=[wide, wide, decay_spec],
        out_specs=[state_spec, row_spec],
        out_shape=[state_shape, row_shape],
        compiler_params=params,
        name="local_states",
    )(k, v, ld)
    decays = decays.reshape(heads, size)
    (prior,) = scan_call(count, local_state, decays, False)
    output, grad_attended, later_local, terms = pl.pallas_call(
        functools.partial(forward_kernel, per, size),
        grid=(steps,),
        in_specs=[wide, wide, wide, wide, decay_spec, gain_spec, state_spec],
        out_specs=[wide, wide, state_spec, row_spec],
        out_shape=[wide_shape, wide_shape, state_shape, row_shape],
        compiler_params=params,
        name="forward",
    )(q, k, v, g, ld, gain, prior)
    later, gain_rows = scan_call(count, later_local, decays, True, terms.reshape(heads, size))
    grad_q, grad_k, grad_v = pl.pallas_call(
        functools.partial(backward_kernel, per, size),
        grid=(steps,),
        in_specs=[wide, wide, wide, wide, decay_spec, state_spec, state_spec],
        out_specs=[wide, wide, wide],
        out_shape=[wide_shape, wide_shape, wide_shape],
        compiler_params=params,
        name="backward",
    )(q, k, v, grad_attended, ld, prior, later)
    share = features // count
    flat_rows = gain_rows.reshape(-1)
    if flat_rows.shape[0] == share:
        grad_gain = flat_rows
    else:
        begin = lax.axis_index("seq") * share % size
        grad_gain = lax.dynamic_slice(flat_rows, (begin,), (share,))
    return tuple(x.reshape(queries.shape) for x in (output, grad_q, grad_k, grad_v)) + (grad_gain,)


def solution(mesh):
    wide = P("dp", "seq", None)
    return jax.shard_map(
        functools.partial(body, mesh.shape["seq"]),
        mesh=mesh,
        in_specs=(wide, wide, wide, wide, P("dp", None, "seq"), P()),
        out_specs=(wide, wide, wide, wide, P("seq")),
        check_vma=False,
    )
```

time: 599 us -> 120 us (0.20)
  waiting for transfers between devices: 388 us -> 0 us
  blocking collectives: 115 us -> 0 us
  Pallas kernels: 0 us -> 114 us
  other arithmetic: 36.4 us -> 0 us
  matrix products: 31.2 us -> 0 us
  starting transfers between devices: 13.2 us -> 0 us
  local copies, waits for them, and re-layouts: 13.4 us -> 5.31 us
    ppermute x11 -> x0, waiting for transfers between devices: 388 us -> none  [partner_2(): return lax.ppermute(value, axis, pairs)]
    pallas_call x0 -> x5, Pallas kernels: none -> 114 us  [the longest x2 72.2 us: scan_call(): pl.pallas_call(functools.partial(scan_kernel, count, group, chunks, rever...]
    unnamed x1 -> x0, blocking collectives: 112 us -> none
    dot_general x12 -> x0, matrix products: 31.2 us -> none  [the longest x1 5.68 us: body(): jnp.einsum('sjhd,sjhe->shde', key_decayed, value_heads, preferred_element...]
    select_n x6 -> x0, other arithmetic: 17.5 us -> none  [pick(): jnp.where(flag, first[1], second[1])]
    ppermute x11 -> x0, starting transfers between devices: 13.2 us -> none  [partner_2(): return lax.ppermute(value, axis, pairs)]
    convert_element_type x2 -> x0, other arithmetic: 8.24 us -> none  [the longest x1 4.73 us: body(): forward_prefix((decay_total, local_state), identity).astype(jnp.bfloat16)]
  transfers between devices with their start and end apart: 11 -> 0, of which waited for: 7 -> 0; matrix products, arithmetic and copies ran while one was open for 3% -> 0% of each run, Pallas kernels for 0% -> 0%
where the time goes in v1:
time: 120 us
  Pallas kernels  114 us (95%)
  local copies, waits for them, and re-layouts  5.31 us (4%)
    pallas_call x2, Pallas kernels, scan_call(): pl.pallas_call(functools.partial(scan_kernel, count, group, chunks, rever...  72.2 us
    pallas_call x1, Pallas kernels, body(): pl.pallas_call(functools.partial(forward_kernel, per, size), grid=(steps,...  19.1 us
    pallas_call x1, Pallas kernels, body(): pl.pallas_call(functools.partial(backward_kernel, per, size), grid=(steps...  15.7 us
    pallas_call x1, Pallas kernels, body(): pl.pallas_call(functools.partial(local_kernel, per, size), grid=(steps,),...  6.73 us
    unnamed x13, local copies, waits for them, and re-layouts  4.54 us

profile of v1, /device:TPU:0, one launch (start us, length us, event | category | flops | bytes accessed | tf_op | source)
XLA Modules:
  0.0 119.7 jit_solution(13950857685058714451)
XLA Ops:
  0.6 0.8 reshape.53.ld_ref
  1.4 0.0 copy-start
  1.4 1.4 %copy-done = bf16[1,192,4096]{2,1,0:T(8,128)(2,1)S(1)} copy-done((bf16[1,192,4096]{2,1,0:T(8,128)(2,1)S(1)}, bf16[1,192,4096]{2,1,0:T(8,128)(2,1)}, u32[]{:S(2)}) %copy-start) | copy-done | bytes 1572888
  2.8 0.0 copy-start.2
  2.8 1.4 %copy-done.2 = bf16[1,192,4096]{2,1,0:T(8,128)(2,1)S(1)} copy-done((bf16[1,192,4096]{2,1,0:T(8,128)(2,1)S(1)}, bf16[1,192,4096]{2,1,0:T(8,128)(2,1)}, u32[]{:S(2)}) %copy-start.2) | copy-done | bytes 1572888
  4.2 6.7 %local_states.1 = (bf16[32,128,128]{2,1,0:T(8,128)(2,1)S(1)}, f32[8,4,128]{2,1,0:T(4,128)S(1)}) custom-call(bf16[192,4096]{1,0:T(8,128)(2,1)S(1)} %bitcast.13, bf16[192,4096]{1,0:T(8,128)(2,1)S(1)} %bitcast.17, f32[8,4,192]{2,1,0:T(4,128)S(1)} %reshape.53.ld_ref), custom_call_target="tpu_custom_call" | custom-call | tf_op jit(solution)/shard_map/local_states/pallas_call | solution.py:347
  11.0 0.0 copy-start.3
  11.0 0.0 copy-start.5
  11.0 33.4 %prefix_scan.1.p_ref = bf16[32,128,128]{2,1,0:T(8,128)(2,1)S(1)} custom-call(bf16[32,128,128]{2,1,0:T(8,128)(2,1)S(1)} %get-tuple-element.16.refs_0_, f32[32,128]{1,0:T(8,128)S(1)} %bitcast.20), custom_call_target="tpu_custom_call" | custom-call | tf_op jit(solution)/shard_map/prefix_scan/pallas_call | solution.py:315
  44.4 0.0 copy-done.3
  44.4 0.0 copy-done.5
  44.4 0.0 copy-start.1
  44.5 19.1 %forward.1 = (bf16[192,4096]{1,0:T(8,128)(2,1)}, bf16[192,4096]{1,0:T(8,128)(2,1)S(1)}, bf16[32,128,128]{2,1,0:T(8,128)(2,1)S(1)}, f32[8,4,128]{2,1,0:T(4,128)S(1)}) custom-call(bf16[192,4096]{1,0:T(8,128)(2,1)S(1)} %bitcast.18, bf16[192,4096]{1,0:T(8,128)(2,1)} %bitcast.12, bf16[192,4096]{1,0:T(8,128)(2,1)} %bitcast.15, bf16[192,4096]{1,0:T(8,128)(2,1)} %bitcast.25, ...), custom_call_target="tpu_custom_call" | custom-call | tf_op jit(solution)/shard_map/forward/pallas_call | solution.py:358
  63.6 0.0 copy-start.4
  63.6 1.1 copy-done.4
  64.7 38.8 %suffix_scan.1 = (bf16[32,128,128]{2,1,0:T(8,128)(2,1)S(1)}, f32[2,128]{1,0:T(2,128)S(1)}) custom-call(bf16[32,128,128]{2,1,0:T(8,128)(2,1)S(1)} %get-tuple-element.20.refs_0_, f32[32,128]{1,0:T(8,128)S(1)} %bitcast.21, f32[32,128]{1,0:T(8,128)S(1)} %bitcast.23), custom_call_target="tpu_custom_call" | custom-call | tf_op jit(solution)/shard_map/suffix_scan/pallas_call | solution.py:315
  103.5 0.0 copy-done.1
  103.5 15.7 %backward.1 = (bf16[192,4096]{1,0:T(8,128)(2,1)}, bf16[192,4096]{1,0:T(8,128)(2,1)}, bf16[192,4096]{1,0:T(8,128)(2,1)}) custom-call(bf16[192,4096]{1,0:T(8,128)(2,1)S(1)} %bitcast.19, bf16[192,4096]{1,0:T(8,128)(2,1)S(1)} %bitcast.14, bf16[192,4096]{1,0:T(8,128)(2,1)} %bitcast.16, bf16[192,4096]{1,0:T(8,128)(2,1)} %copy-done.4, ...), custom_call_target="tpu_custom_call" | custom-call | tf_op jit(solution)/shard_map/backward/pallas_call | solution.py:368
  119.2 0.6 copy.12
Async XLA Ops:
  1.4 1.4 %copy-start = (bf16[1,192,4096]{2,1,0:T(8,128)(2,1)S(1)}, bf16[1,192,4096]{2,1,0:T(8,128)(2,1)}, u32[]{:S(2)}) copy-start(bf16[1,192,4096]{2,1,0:T(8,128)(2,1)} %param.7) | copy-start | bytes 4718596
  2.8 1.4 %copy-start.2 = (bf16[1,192,4096]{2,1,0:T(8,128)(2,1)S(1)}, bf16[1,192,4096]{2,1,0:T(8,128)(2,1)}, u32[]{:S(2)}) copy-start(bf16[1,192,4096]{2,1,0:T(8,128)(2,1)} %param.8) | copy-start | bytes 4718596
  11.0 33.5 %copy-start.3 = (bf16[1,192,4096]{2,1,0:T(8,128)(2,1)S(1)}, bf16[1,192,4096]{2,1,0:T(8,128)(2,1)}, u32[]{:S(2)}) copy-start(bf16[1,192,4096]{2,1,0:T(8,128)(2,1)} %param.6) | copy-start | bytes 4718596
  11.0 33.5 %copy-start.5 = (f32[4096]{0:T(1024)S(1)}, f32[4096]{0:T(1024)}, u32[]{:S(2)}) copy-start(f32[4096]{0:T(1024)} %param.11) | copy-start | bytes 49156
  44.4 59.0 %copy-start.1 = (bf16[1,192,4096]{2,1,0:T(8,128)(2,1)S(1)}, bf16[1,192,4096]{2,1,0:T(8,128)(2,1)}, u32[]{:S(2)}) copy-start(bf16[1,192,4096]{2,1,0:T(8,128)(2,1)} %param.7) | copy-start | bytes 4718596
  63.6 1.1 copy-start.4

commit v2 on v0

v2 whole, which is shorter than its diff:
```python
import functools

import jax
import jax.numpy as jnp
from jax import lax
from jax.experimental import pallas as pl
from jax.experimental.pallas import tpu as pltpu
from jax.sharding import PartitionSpec as P

epsilon = 1e-06
F32 = jnp.float32
BF16 = jnp.bfloat16
MESH = pl.DeviceIdType.MESH
NEG = -1e30


def dot_nn(a, b):
    return lax.dot_general(a, b, (((1,), (0,)), ((), ())), preferred_element_type=F32)


def dot_nt(a, b):
    return lax.dot_general(a, b, (((1,), (1,)), ((), ())), preferred_element_type=F32)


def dot_tn(a, b):
    return lax.dot_general(a, b, (((0,), (0,)), ((), ())), preferred_element_type=F32)


def cumulative(ld):
    tokens = ld.shape[1]
    i = lax.broadcasted_iota(jnp.int32, (tokens, tokens), 0)
    j = lax.broadcasted_iota(jnp.int32, (tokens, tokens), 1)
    lower = (i >= j).astype(F32)
    exact = lax.Precision.HIGHEST
    rows = lax.dot_general(
        ld, lower, (((1,), (1,)), ((), ())), precision=exact, preferred_element_type=F32
    )
    columns = lax.dot_general(
        lower, ld, (((1,), (1,)), ((), ())), precision=exact, preferred_element_type=F32
    )
    return rows, columns, i >= j


def fused_kernel(
    count, group, chunks,
    q_hbm, k_hbm, v_hbm, g_hbm, ld_ref, gain_ref,
    out_ref, gq_ref, gk_ref, gv_ref, sum_ref,
    q_ref, k_ref, v_ref, g_ref, ga_ref, weighted_ref, weight_ref, inside_ref,
    pk_ref, pv_ref, col_ref, row_ref, start_ref, end_ref, decay_ref, decay_got, term_ref, gain_got,
    local, got, given, carry_in, carry_out, state,
    in_sem, dec_send, dec_recv, gain_send, gain_recv,
    got_send, got_recv, car_send, car_recv, ret_send, ret_recv,
):
    me = lax.axis_index("seq")
    dp = lax.axis_index("dp")
    planes = count // group
    mine = lax.rem(me, group)
    plane = me // group
    heads, tokens = ld_ref.shape
    size = q_ref.shape[1] // heads
    owned = heads // group
    piece = owned // chunks
    width = piece * size
    FORWARD, BACKWARD = 0, 1

    loads = [
        pltpu.make_async_copy(src, dst, in_sem.at[n])
        for n, (src, dst) in enumerate(
            ((k_hbm, k_ref), (v_hbm, v_ref), (q_hbm, q_ref), (g_hbm, g_ref))
        )
    ]
    for load in loads:
        load.start()

    rows, columns, causal = cumulative(ld_ref[...])
    last = columns[tokens - 1 :, :]
    start, end = jnp.exp(columns), jnp.exp(last - columns)
    decay_ref[...] = jnp.broadcast_to(jnp.exp(rows[:, tokens - 1 :]), (heads, size))
    for n in range(heads // piece):
        part = slice(n * piece, (n + 1) * piece)
        col_ref[n] = columns[:, part]
        start_ref[n] = start[:, part]
        end_ref[n] = end[:, part]
        row_ref[n] = rows[part, :]

    def to_device(src, dst, send, recv, target):
        return pltpu.make_async_remote_copy(
            src_ref=src, dst_ref=dst, send_sem=send, recv_sem=recv,
            device_id=(target, dp), device_id_type=MESH,
        )

    def ahead(offset):
        return lax.rem(mine + offset, group)

    def behind(offset):
        return lax.rem(mine + group - offset, group)

    def owned_rows(peer, chunk):
        return pl.ds(peer * owned + chunk * piece, piece)

    def chunk_rows(chunk):
        return pl.ds(chunk * piece, piece)

    def locals_of(way, offset, chunk, owner, slot, target):
        return to_device(
            local.at[way, owned_rows(owner, chunk)],
            got.at[way, slot, chunk_rows(chunk)],
            got_send.at[way, offset, chunk],
            got_recv.at[way, offset, chunk],
            plane * group + target,
        )

    def give_local(way, offset, chunk):
        return locals_of(way, offset, chunk, ahead(offset), mine, ahead(offset))

    def take_local(way, offset, chunk):
        return locals_of(way, offset, chunk, mine, behind(offset), behind(offset))

    def returns_of(way, offset, chunk, slot, owner, target):
        return to_device(
            given.at[way, slot, chunk_rows(chunk)],
            state.at[way, owned_rows(owner, chunk)],
            ret_send.at[way, offset, chunk],
            ret_recv.at[way, offset, chunk],
            plane * group + target,
        )

    def give_back(way, offset, chunk):
        return returns_of(way, offset, chunk, ahead(offset), mine, ahead(offset))

    def take_back(way, offset, chunk):
        return returns_of(way, offset, chunk, mine, behind(offset), behind(offset))

    def decays_of(offset, owner, slot, target):
        return to_device(
            decay_ref.at[pl.ds(owner * owned, owned)],
            decay_got.at[slot],
            dec_send.at[offset],
            dec_recv.at[offset],
            plane * group + target,
        )

    def carry(way, chunk):
        step = 1 if way == FORWARD else planes - 1
        return to_device(
            carry_out.at[way, chunk_rows(chunk)],
            carry_in.at[way, chunk_rows(chunk)],
            car_send.at[way, chunk],
            car_recv.at[way, chunk],
            lax.rem(plane + step, planes) * group + mine,
        )

    lowest, highest = plane == 0, plane == planes - 1
    first = (lowest, highest)
    final = (highest, lowest)

    def send_locals(way, chunk):
        for offset in range(1, group):
            give_local(way, offset, chunk).start()
        got[way, mine, chunk_rows(chunk)] = local[way, owned_rows(mine, chunk)]

    def combine_chunk(way, chunk):
        for offset in range(1, group):
            take_local(way, offset, chunk).wait_recv()

        @pl.when(jnp.logical_not(first[way]))
        def _():
            carry(way, chunk).wait_recv()

        order = list(range(group))
        if way == BACKWARD:
            order = order[::-1]
        for n in range(piece):
            h = chunk * piece + n
            value = carry_in[way, h].astype(F32)
            for g in order:
                given[way, g, h] = value.astype(BF16)
                value = decay_got[g, pl.ds(h, 1)] * value + got[way, g, h].astype(F32)
            carry_out[way, h] = value.astype(BF16)

        @pl.when(jnp.logical_not(final[way]))
        def _():
            carry(way, chunk).start()

        for offset in range(1, group):
            give_back(way, offset, chunk).start()
        state[way, owned_rows(mine, chunk)] = given[way, mine, chunk_rows(chunk)]

    def wait_states(way, chunk):
        for offset in range(1, group):
            take_back(way, offset, chunk).wait_recv()

    def each_head(chunk, act):
        both = 2 if group % 2 == 0 else 1

        def step(pair, unused):
            for half in range(both):
                owner = pair * both + half
                n = owner * chunks + chunk
                for h in range(piece):
                    head = owner * owned + chunk * piece + h
                    cols = pl.ds(pl.multiple_of(head * size, size), size)
                    act(head, cols, n, slice(h, h + 1))
            return unused

        lax.fori_loop(0, group // both, step, 0)

    def local_act(head, cols, n, h):
        kd = (k_ref[:, cols].astype(F32) * end_ref[n][:, h]).astype(BF16)
        local[FORWARD, head] = dot_tn(kd, v_ref[:, cols]).astype(BF16)

    def inside_act(head, cols, n, h):
        weight = jnp.exp(jnp.where(causal, col_ref[n][:, h] - row_ref[n][h, :], NEG))
        weighted = (dot_nt(q_ref[:, cols], k_ref[:, cols]) * weight).astype(BF16)
        weight_ref[head] = weight
        weighted_ref[head] = weighted
        inside_ref[:, cols] = dot_nn(weighted, v_ref[:, cols])

    def attend_act(head, cols, n, h):
        q = q_ref[:, cols]
        begin = start_ref[n][:, h]
        attended = inside_ref[:, cols] + dot_nn(q, state[FORWARD, head]) * begin
        inv = lax.rsqrt(jnp.mean(attended * attended, axis=1, keepdims=True) + epsilon)
        normed = attended * inv
        gain = gain_ref[:, cols]
        out_ref[:, cols] = (normed * gain).astype(BF16)
        g = g_ref[:, cols].astype(F32)
        term_ref[pl.ds(head, 1), :] = jnp.sum(g * normed, axis=0, keepdims=True)
        scaled = g * gain
        ga = (inv * (scaled - normed * jnp.mean(scaled * normed, axis=1, keepdims=True))).astype(BF16)
        ga_ref[:, cols] = ga
        qd = (q.astype(F32) * begin).astype(BF16)
        local[BACKWARD, head] = dot_tn(qd, ga).astype(BF16)

    def grad_act(head, cols, n, h):
        q, k, v, ga = q_ref[:, cols], k_ref[:, cols], v_ref[:, cols], ga_ref[:, cols]
        gw = (dot_nt(ga, v) * weight_ref[head]).astype(BF16)
        begin = start_ref[n][:, h]
        gq_ref[:, cols] = (dot_nn(gw, k) + begin * dot_nt(ga, state[FORWARD, head])).astype(BF16)
        pk_ref[:, cols] = dot_tn(gw, q)
        pv_ref[:, cols] = dot_tn(weighted_ref[head], ga)

    def finish_act(head, cols, n, h):
        finish = end_ref[n][:, h]
        later = state[BACKWARD, head]
        gk_ref[:, cols] = (pk_ref[:, cols] + finish * dot_nt(v_ref[:, cols], later)).astype(BF16)
        gv_ref[:, cols] = (pv_ref[:, cols] + finish * dot_nn(k_ref[:, cols], later)).astype(BF16)

    def over(low, high, act):
        def step(chunk, unused):
            act(chunk)
            return unused

        lax.fori_loop(low, high, step, 0)

    for offset in range(1, group):
        decays_of(offset, ahead(offset), mine, ahead(offset)).start()
    decay_got[mine] = decay_ref[pl.ds(mine * owned, owned)]

    @pl.when(lowest)
    def _():
        carry_in[FORWARD] = jnp.zeros(carry_in.shape[1:], BF16)

    @pl.when(highest)
    def _():
        carry_in[BACKWARD] = jnp.zeros(carry_in.shape[1:], BF16)

    loads[0].wait()
    loads[1].wait()

    def local_chunk(chunk):
        each_head(chunk, local_act)
        send_locals(FORWARD, chunk)

    over(0, chunks, local_chunk)
    loads[2].wait()
    for offset in range(1, group):
        decays_of(offset, mine, behind(offset), behind(offset)).wait_recv()

    before = plane * chunks // planes

    def prefix_step(j):
        low = jnp.where(j == 0, 0, jnp.minimum(before + j - 1, chunks))
        high = jnp.where(j == chunks, chunks, jnp.minimum(before + j, chunks))
        over(low, high, lambda chunk: each_head(chunk, inside_act))

        @pl.when(j < chunks)
        def _():
            combine_chunk(FORWARD, j)

    over(0, chunks + 1, prefix_step)
    loads[3].wait()

    def attend_chunk(chunk):
        wait_states(FORWARD, chunk)
        each_head(chunk, attend_act)
        send_locals(BACKWARD, chunk)

    ahead_of = jnp.where(highest, chunks - 1, chunks)
    from_top = planes - 1 - plane
    early = jnp.minimum(from_top * chunks // max(planes - 1, 1), chunks)

    def suffix_step(j):
        over(
            jnp.where(j == 0, 0, jnp.where(j == 1, ahead_of, chunks)),
            jnp.where(j == 0, ahead_of, chunks),
            attend_chunk,
        )
        low = jnp.where(j == 0, 0, jnp.minimum(early + jnp.maximum(j - 2, 0), chunks))
        high = jnp.where(j == chunks, chunks, jnp.minimum(early + jnp.maximum(j - 1, 0), chunks))
        over(low, high, lambda chunk: each_head(chunk, grad_act))

        @pl.when(j < chunks)
        def _():
            combine_chunk(BACKWARD, j)

    over(0, chunks + 1, suffix_step)

    share = gain_got.shape[1]
    total = 2 * count
    flat = me * 2 + dp

    def send_gain(offset, unused):
        there = lax.rem(flat + offset, total)
        pltpu.make_async_remote_copy(
            src_ref=term_ref.at[pl.ds((there // 2) * heads // count, share)],
            dst_ref=gain_got.at[offset - 1],
            send_sem=gain_send,
            recv_sem=gain_recv,
            device_id=(there // 2, lax.rem(there, 2)),
            device_id_type=MESH,
        ).start()
        return unused

    lax.fori_loop(1, total, send_gain, 0)

    def finish_chunk(chunk):
        wait_states(BACKWARD, chunk)
        each_head(chunk, finish_act)

    over(0, chunks, finish_chunk)

    pltpu.make_async_copy(gain_got, gain_got, gain_recv).wait()
    pltpu.make_async_copy(gain_got, gain_got, gain_send).wait()
    sum_ref[...] = jnp.sum(gain_got[...], axis=0) + term_ref[pl.ds(me * heads // count, share)]

    def drain(chunk):
        for way in (FORWARD, BACKWARD):
            for offset in range(1, group):
                give_local(way, offset, chunk).wait_send()
                give_back(way, offset, chunk).wait_send()

            @pl.when(jnp.logical_not(final[way]))
            def _():
                carry(way, chunk).wait_send()

    over(0, chunks, drain)
    for offset in range(1, group):
        decays_of(offset, ahead(offset), mine, ahead(offset)).wait_send()


def body(count, queries, key_vectors, value_vectors, out_grad, log_decay, norm_gain):
    _, tokens, features = queries.shape
    heads = log_decay.shape[1]
    size = features // heads
    group = 1 << (count.bit_length() // 2)
    owned = heads // group
    chunks = min(owned, 4)
    piece = owned // chunks
    share = max(1, heads // count)
    q, k, v, g = (x.reshape(tokens, features) for x in (queries, key_vectors, value_vectors, out_grad))
    vmem = pl.BlockSpec(memory_space=pltpu.VMEM)
    anywhere = pl.BlockSpec(memory_space=pl.ANY)
    dma = pltpu.SemaphoreType.DMA
    wide = (tokens, features)
    states = (2, owned, size, size)
    exchange = (2, group, owned, size, size)
    whole = jax.ShapeDtypeStruct(wide, BF16)
    output, grad_q, grad_k, grad_v, gain_rows = pl.pallas_call(
        functools.partial(fused_kernel, count, group, chunks),
        out_shape=[whole] * 4 + [jax.ShapeDtypeStruct((share, size), F32)],
        in_specs=[anywhere] * 4 + [vmem] * 2,
        out_specs=[vmem] * 5,
        scratch_shapes=[pltpu.VMEM(wide, BF16)] * 5
        + [
            pltpu.VMEM((heads, tokens, tokens), BF16),
            pltpu.VMEM((heads, tokens, tokens), F32),
            pltpu.VMEM(wide, F32),
            pltpu.VMEM(wide, F32),
            pltpu.VMEM(wide, F32),
            pltpu.VMEM((heads // piece, tokens, piece), F32),
            pltpu.VMEM((heads // piece, piece, tokens), F32),
            pltpu.VMEM((heads // piece, tokens, piece), F32),
            pltpu.VMEM((heads // piece, tokens, piece), F32),
            pltpu.VMEM((heads, size), F32),
            pltpu.VMEM((group, owned, size), F32),
            pltpu.VMEM((heads, size), F32),
            pltpu.VMEM((2 * count - 1, share, size), F32),
            pltpu.VMEM((2, heads, size, size), BF16),
            pltpu.VMEM(exchange, BF16),
            pltpu.VMEM(exchange, BF16),
            pltpu.VMEM(states, BF16),
            pltpu.VMEM(states, BF16),
            pltpu.VMEM((2, heads, size, size), BF16),
            dma((4,)),
            dma((group,)),
            dma((group,)),
            dma,
            dma,
            dma((2, group, chunks)),
            dma((2, group, chunks)),
            dma((2, chunks)),
            dma((2, chunks)),
            dma((2, group, chunks)),
            dma((2, group, chunks)),
        ],
        compiler_params=pltpu.CompilerParams(
            has_side_effects=True, vmem_limit_bytes=54 * 1024 * 1024
        ),
        name="fused",
    )(q, k, v, g, log_decay.reshape(heads, tokens), norm_gain.reshape(1, features))
    part = features // count
    flat_rows = gain_rows.reshape(-1)
    if flat_rows.shape[0] == part:
        grad_gain = flat_rows
    else:
        begin = lax.axis_index("seq") * part % size
        grad_gain = lax.dynamic_slice(flat_rows, (begin,), (part,))
    return tuple(x.reshape(queries.shape) for x in (output, grad_q, grad_k, grad_v)) + (grad_gain,)


def solution(mesh):
    wide = P("dp", "seq", None)
    return jax.shard_map(
        functools.partial(body, mesh.shape["seq"]),
        mesh=mesh,
        in_specs=(wide, wide, wide, wide, P("dp", None, "seq"), P()),
        out_specs=(wide, wide, wide, wide, P("seq")),
        check_vma=False,
    )
```

time: 599 us -> 85.2 us (0.14)
  waiting for transfers between devices: 388 us -> 0 us
  blocking collectives: 115 us -> 0 us
  Pallas kernels: 0 us -> 75.8 us
  other arithmetic: 36.4 us -> 0 us
  matrix products: 31.2 us -> 0 us
  starting transfers between devices: 13.2 us -> 0 us
    ppermute x11 -> x0, waiting for transfers between devices: 388 us -> none  [partner_2(): return lax.ppermute(value, axis, pairs)]
    unnamed x1 -> x0, blocking collectives: 112 us -> none
    pallas_call x0 -> x1, Pallas kernels: none -> 75.8 us  [body(): pl.pallas_call(functools.partial(fused_kernel, count, group, chunks), out...]
    dot_general x12 -> x0, matrix products: 31.2 us -> none  [the longest x1 5.68 us: body(): jnp.einsum('sjhd,sjhe->shde', key_decayed, value_heads, preferred_element...]
    select_n x6 -> x0, other arithmetic: 17.5 us -> none  [pick(): jnp.where(flag, first[1], second[1])]
    ppermute x11 -> x0, starting transfers between devices: 13.2 us -> none  [partner_2(): return lax.ppermute(value, axis, pairs)]
    convert_element_type x2 -> x0, other arithmetic: 8.24 us -> none  [the longest x1 4.73 us: body(): forward_prefix((decay_total, local_state), identity).astype(jnp.bfloat16)]
  transfers between devices with their start and end apart: 11 -> 0, of which waited for: 7 -> 0; matrix products, arithmetic and copies ran while one was open for 3% -> 0% of each run, Pallas kernels for 0% -> 0%
where the time goes in v2:
time: 85.2 us; the launch traced here: 84.9 us
  Pallas kernels  75.8 us (89%)
  local copies, waits for them, and re-layouts  8.48 us (10%)
    pallas_call x1, Pallas kernels, body(): pl.pallas_call(functools.partial(fused_kernel, count, group, chunks), out...  75.8 us
    unnamed x13, local copies, waits for them, and re-layouts  8.48 us

profile of v2, /device:TPU:0, one launch (start us, length us, event | category | flops | bytes accessed | tf_op | source)
XLA Modules:
  0.0 84.9 jit_solution(13167727615897171422)
XLA Ops:
  0.6 75.8 %fused.1 = (bf16[192,4096]{1,0:T(8,128)(2,1)}, bf16[192,4096]{1,0:T(8,128)(2,1)}, bf16[192,4096]{1,0:T(8,128)(2,1)}, bf16[192,4096]{1,0:T(8,128)(2,1)}, f32[2,128]{1,0:T(2,128)}) custom-call(bf16[192,4096]{1,0:T(8,128)(2,1)} %bitcast.15, bf16[192,4096]{1,0:T(8,128)(2,1)} %bitcast.16, bf16[192,4096]{1,0:T(8,128)(2,1)} %bitcast.17, ...), custom_call_target="tpu_custom_call" | custom-call | tf_op jit(solution)/shard_map/fused/pallas_call | solution.py:379
  76.4 0.0 copy-start.2
  76.5 2.8 %copy.16 = bf16[1,192,4096]{2,1,0:T(8,128)(2,1)} copy(bf16[1,192,4096]{2,1,0:T(8,128)(2,1)} %bitcast.14) | data formatting | bytes 3145728
  79.3 0.0 copy-done.2
  79.3 0.0 copy-start.1
  79.3 1.1 %copy.17 = bf16[1,192,4096]{2,1,0:T(8,128)(2,1)} copy(bf16[1,192,4096]{2,1,0:T(8,128)(2,1)S(1)} %bitcast.13) | data formatting | bytes 3145728
  80.4 0.8 copy-done.1
  81.3 0.0 copy-start
  81.3 1.1 %copy.18 = bf16[1,192,4096]{2,1,0:T(8,128)(2,1)} copy(bf16[1,192,4096]{2,1,0:T(8,128)(2,1)S(1)} %bitcast.12) | data formatting | bytes 3145728
  82.4 0.8 copy-done
  83.2 0.0 copy-start.3
  83.2 1.1 %copy.19 = bf16[1,192,4096]{2,1,0:T(8,128)(2,1)} copy(bf16[1,192,4096]{2,1,0:T(8,128)(2,1)S(1)} %bitcast.11) | data formatting | bytes 3145728
  84.4 0.0 copy-done.3
  84.4 0.6 copy.20
Async XLA Ops:
  76.4 2.8 %copy-start.2 = (bf16[192,4096]{1,0:T(8,128)(2,1)S(1)}, bf16[192,4096]{1,0:T(8,128)(2,1)}, u32[]{:S(2)}) copy-start(bf16[192,4096]{1,0:T(8,128)(2,1)} %get-tuple-element.11) | copy-start | bytes 4718596
  79.3 2.0 %copy-start.1 = (bf16[192,4096]{1,0:T(8,128)(2,1)S(1)}, bf16[192,4096]{1,0:T(8,128)(2,1)}, u32[]{:S(2)}) copy-start(bf16[192,4096]{1,0:T(8,128)(2,1)} %get-tuple-element.12) | copy-start | bytes 4718596
  81.3 2.0 %copy-start = (bf16[192,4096]{1,0:T(8,128)(2,1)S(1)}, bf16[192,4096]{1,0:T(8,128)(2,1)}, u32[]{:S(2)}) copy-start(bf16[192,4096]{1,0:T(8,128)(2,1)} %get-tuple-element.13) | copy-start | bytes 4718596
  83.2 1.1 %copy-start.3 = (f32[2,128]{1,0:T(2,128)S(1)}, f32[2,128]{1,0:T(2,128)}, u32[]{:S(2)}) copy-start(f32[2,128]{1,0:T(2,128)} %get-tuple-element.14) | copy-start | bytes 3076

commit v3 on v2

--- a/solution.py
+++ b/solution.py
@@ -46,7 +46,7 @@
     q_hbm, k_hbm, v_hbm, g_hbm, ld_ref, gain_ref,
     out_ref, gq_ref, gk_ref, gv_ref, sum_ref,
     q_ref, k_ref, v_ref, g_ref, ga_ref, weighted_ref, weight_ref, inside_ref,
-    pk_ref, pv_ref, col_ref, row_ref, start_ref, end_ref, decay_ref, decay_got, term_ref, gain_got,
+    pv_ref, col_ref, row_ref, start_ref, end_ref, decay_ref, decay_got, term_ref, gain_got,
     local, got, given, carry_in, carry_out, state,
     in_sem, dec_send, dec_recv, gain_send, gain_recv,
     got_send, got_recv, car_send, car_recv, ret_send, ret_recv,
@@ -191,7 +191,7 @@
             take_back(way, offset, chunk).wait_recv()
 
     def each_head(chunk, act):
-        both = 2 if group % 2 == 0 else 1
+        both = min(group, max(1, 4 // piece))
 
         def step(pair, unused):
             for half in range(both):
@@ -237,13 +237,13 @@
         gw = (dot_nt(ga, v) * weight_ref[head]).astype(BF16)
         begin = start_ref[n][:, h]
         gq_ref[:, cols] = (dot_nn(gw, k) + begin * dot_nt(ga, state[FORWARD, head])).astype(BF16)
-        pk_ref[:, cols] = dot_tn(gw, q)
+        inside_ref[:, cols] = dot_tn(gw, q)
         pv_ref[:, cols] = dot_tn(weighted_ref[head], ga)
 
     def finish_act(head, cols, n, h):
         finish = end_ref[n][:, h]
         later = state[BACKWARD, head]
-        gk_ref[:, cols] = (pk_ref[:, cols] + finish * dot_nt(v_ref[:, cols], later)).astype(BF16)
+        gk_ref[:, cols] = (inside_ref[:, cols] + finish * dot_nt(v_ref[:, cols], later)).astype(BF16)
         gv_ref[:, cols] = (pv_ref[:, cols] + finish * dot_nn(k_ref[:, cols], later)).astype(BF16)
 
     def over(low, high, act):
@@ -296,14 +296,14 @@
         each_head(chunk, attend_act)
         send_locals(BACKWARD, chunk)
 
-    ahead_of = jnp.where(highest, chunks - 1, chunks)
     from_top = planes - 1 - plane
+    lead = 3 + 2 * from_top
     early = jnp.minimum(from_top * chunks // max(planes - 1, 1), chunks)
 
     def suffix_step(j):
         over(
-            jnp.where(j == 0, 0, jnp.where(j == 1, ahead_of, chunks)),
-            jnp.where(j == 0, ahead_of, chunks),
+            jnp.where(j == 0, 0, jnp.minimum(j - 1 + lead, chunks)),
+            jnp.minimum(j + lead, chunks),
             attend_chunk,
         )
         low = jnp.where(j == 0, 0, jnp.minimum(early + jnp.maximum(j - 2, 0), chunks))
@@ -365,12 +365,12 @@
     size = features // heads
     group = 1 << (count.bit_length() // 2)
     owned = heads // group
-    chunks = min(owned, 4)
+    chunks = min(owned, 8)
     piece = owned // chunks
     share = max(1, heads // count)
     q, k, v, g = (x.reshape(tokens, features) for x in (queries, key_vectors, value_vectors, out_grad))
     vmem = pl.BlockSpec(memory_space=pltpu.VMEM)
-    anywhere = pl.BlockSpec(memory_space=pl.ANY)
+    anywhere = pl.BlockSpec(memory_space=pltpu.HBM)
     dma = pltpu.SemaphoreType.DMA
     wide = (tokens, features)
     states = (2, owned, size, size)
@@ -385,7 +385,6 @@
         + [
             pltpu.VMEM((heads, tokens, tokens), BF16),
             pltpu.VMEM((heads, tokens, tokens), F32),
-            pltpu.VMEM(wide, F32),
             pltpu.VMEM(wide, F32),
             pltpu.VMEM(wide, F32),
             pltpu.VMEM((heads // piece, tokens, piece), F32),
@@ -415,7 +414,7 @@
             dma((2, group, chunks)),
         ],
         compiler_params=pltpu.CompilerParams(
-            has_side_effects=True, vmem_limit_bytes=54 * 1024 * 1024
+            has_side_effects=True, vmem_limit_bytes=47 * 1024 * 1024
         ),
         name="fused",
     )(q, k, v, g, log_decay.reshape(heads, tokens), norm_gain.reshape(1, features))

time: 85.2 us -> 80.4 us (0.944)
  Pallas kernels: 75.8 us -> 72.9 us
  local copies, waits for them, and re-layouts: 8.48 us -> 6.6 us
    pallas_call x1, Pallas kernels: 75.8 us -> 72.9 us  [body(): pl.pallas_call(functools.partial(fused_kernel, count, group, chunks), out...]
    unnamed x13 -> x9, local copies, waits for them, and re-layouts: 8.48 us -> 6.6 us
where the time goes in v3:
time: 80.4 us; the launch traced here: 80.2 us
  Pallas kernels  72.9 us (91%)
  local copies, waits for them, and re-layouts  6.6 us (8%)
    pallas_call x1, Pallas kernels, body(): pl.pallas_call(functools.partial(fused_kernel, count, group, chunks), out...  72.9 us
    unnamed x9, local copies, waits for them, and re-layouts  6.6 us

profile of v3, /device:TPU:0, one launch (start us, length us, event | category | flops | bytes accessed | tf_op | source)
XLA Modules:
  0.0 80.2 jit_solution(18368337853857207941)
XLA Ops:
  0.6 0.0 copy-start
  0.6 0.7 copy-done
  1.4 0.0 copy-start.1
  1.4 0.7 copy-done.1
  2.1 72.9 %fused.1 = (bf16[192,4096]{1,0:T(8,128)(2,1)S(1)}, bf16[192,4096]{1,0:T(8,128)(2,1)S(1)}, bf16[192,4096]{1,0:T(8,128)(2,1)S(1)}, bf16[192,4096]{1,0:T(8,128)(2,1)S(1)}, f32[2,128]{1,0:T(2,128)S(1)}) custom-call(bf16[192,4096]{1,0:T(8,128)(2,1)} %bitcast.18, bf16[192,4096]{1,0:T(8,128)(2,1)} %bitcast.19, bf16[192,4096]{1,0:T(8,128)(2,1)} %bitcast.20, ...), custom_call_target="tpu_custom_call" | custom-call | tf_op jit(solution)/shard_map/fused/pallas_call | solution.py:379
  75.1 1.1 %copy.16 = bf16[1,192,4096]{2,1,0:T(8,128)(2,1)} copy(bf16[1,192,4096]{2,1,0:T(8,128)(2,1)S(1)} %bitcast.14) | data formatting | bytes 3145728
  76.2 1.1 %copy.17 = bf16[1,192,4096]{2,1,0:T(8,128)(2,1)} copy(bf16[1,192,4096]{2,1,0:T(8,128)(2,1)S(1)} %bitcast.13) | data formatting | bytes 3145728
  77.3 1.1 %copy.18 = bf16[1,192,4096]{2,1,0:T(8,128)(2,1)} copy(bf16[1,192,4096]{2,1,0:T(8,128)(2,1)S(1)} %bitcast.12) | data formatting | bytes 3145728
  78.5 1.1 %copy.19 = bf16[1,192,4096]{2,1,0:T(8,128)(2,1)} copy(bf16[1,192,4096]{2,1,0:T(8,128)(2,1)S(1)} %bitcast.11) | data formatting | bytes 3145728
  79.6 0.6 copy.20
Async XLA Ops:
  0.6 0.8 copy-start
  1.4 0.7 copy-start.1
